TPU v7x, 32 devices: a whole 2x2x4 slice. The times are simulated.
32 devices in a mesh: tm: 32 (over z, y, x, core).
Axes of the slice: x: 2, y: 2, z: 4, core: 2. Of those that a mesh axis runs over, the one named last changes fastest.
Arguments:
- samples: int32 [65536, 128], P('tm'), may hold values from -8 to 7
Outputs:
- spectra: float32 [2, 128, 16384], P(None, None, 'tm')
All inputs are finite; a program needn't handle non-finite values.
Results may differ from a plain program's by a relative error of at most 0.0003.
Values may be sent and summed in bfloat16 or wider, within the bound.
A program may use at most 192 MiB of HBM per device.

v0:
```python
import functools

import jax
import jax.numpy as jnp
import numpy as np
from jax import lax
from jax.experimental import pallas as pl
from jax.experimental.pallas import tpu as pltpu
from jax.sharding import PartitionSpec as P

LAGS = 128
Q = 16
JS = 16
TAUS = LAGS + Q
OUT_ROWS = (LAGS + 1) * JS
TILE = OUT_ROWS // 3
MESH = pl.DeviceIdType.MESH


def flipped(value, mask):
    out = 0
    bit = 1
    while bit <= 64:
        b = (value // bit) % 2
        out = out + ((b + (1 if mask & bit else 0)) % 2) * bit
        bit *= 2
    return out


def code_levels(limit):
    for m in range(8192, 128, -128):
        steps = [m * e + limit / 2**e for e in range(20)]
        if min(steps) <= 32700:
            return m, int(np.argmin(steps)) + 1


def encoded(value, m, levels):
    size = jnp.abs(value)
    code = size
    for e in range(1, levels):
        code = jnp.minimum(code, size * 0.5**e + float(m * e))
    code = (code + 0.5).astype(jnp.int32)
    return jnp.where(value < 0, -code, code).astype(jnp.int16)


def decoded(code, m, levels):
    code = code.astype(jnp.int32).astype(jnp.float32)
    size = jnp.abs(code)
    value = size
    for e in range(1, levels):
        value = jnp.maximum(value, (size - float(m * e)) * 2.0**e)
    return jnp.where(code < 0, -value, value)


def kernel(n, T, G, mj, iw, samples, perm, out, vbuf, ts, tb, ut, acc, sbuf, rbuf,
           send_v, recv_v, send_t, recv_t, send_h, send_r, recv_r):
    me = lax.axis_index("tm")
    g = me % G
    t = me // G
    core = g % 2
    base = t * G
    rows = samples.shape[0]
    R = rows // Q
    C = G // 2
    half = Q // 4
    m_code, levels = code_levels(rows * G * 64)

    barrier = pltpu.get_barrier_semaphore()

    def greet(device):
        pl.semaphore_signal(barrier, inc=1, device_id=(device,), device_id_type=MESH)

    for k in range(1, G):
        greet(base + flipped(g, k))
    for k in range(1, T):
        greet((t + k) % T * G + g)

    @pl.when(t < T - 1)
    def _():
        greet(base + G)

    for q in range(Q):
        phase = samples[pl.ds(q, R, stride=Q), :].astype(jnp.float32).astype(jnp.bfloat16)
        vbuf[g, q // 2, :, (q % 2) * 128:(q % 2 + 1) * 128] = phase

    feeds = jnp.logical_and(g == 0, t > 0)
    pl.semaphore_wait(barrier, jnp.where(feeds, 2 * G + T - 2, G + T - 2))

    def copy_t(k):
        d = flipped(g, k)
        return pltpu.make_async_remote_copy(
            src_ref=ts.at[d], dst_ref=tb.at[g], send_sem=send_t.at[k], recv_sem=recv_t.at[g],
            device_id=(base + d,), device_id_type=MESH)

    def copy_h(d):
        return pltpu.make_async_remote_copy(
            src_ref=ts.at[d], dst_ref=tb.at[G], send_sem=send_h.at[d], recv_sem=recv_t.at[G],
            device_id=(base - G + d,), device_id_type=MESH)

    def copy_v(slot, d, h, sem):
        part = vbuf.at[slot, pl.ds(h * half, half)]
        return pltpu.make_async_remote_copy(
            src_ref=part, dst_ref=part, send_sem=send_v.at[sem, h],
            recv_sem=recv_v.at[slot, h], device_id=(base + d,), device_id_type=MESH)

    partner = flipped(g, 1)
    relay = C == 4
    sends = []

    def send(*what):
        copy_v(*what).start()
        sends.append(what)

    if relay:
        send(g, flipped(g, 2), 1, 1)
        send(g, flipped(g, 4), 0, 2)

    for q in range(Q):
        turned = lax.dot_general(
            perm[...], vbuf[g, q // 2, :, (q % 2) * 128:(q % 2 + 1) * 128],
            (((1,), (1,)), ((), ())), preferred_element_type=jnp.float32
        ).astype(jnp.bfloat16)
        for d in range(G):
            ts[d, q * JS:(q + 1) * JS, :] = turned[d * JS:(d + 1) * JS, :]

    for k in range(G - 1, 0, -1):
        copy_t(k).start()

    @pl.when(jnp.logical_and(g == 0, t > 0))
    def _():
        for d in range(G):
            copy_h(d).start()

    if relay:
        send(g, flipped(g, 2), 0, 1)
        send(g, flipped(g, 4), 1, 2)
    else:
        for c in range(1, C):
            for h in range(2):
                send(g, flipped(g, 2 * c), h, c)
    for h in range(2):
        send(g, partner, h, 0)

    tb[g] = ts[g]

    @pl.when(t == T - 1)
    def _():
        tb[G] = jnp.zeros(tb.shape[1:], tb.dtype)

    @pl.when(t < T - 1)
    def _():
        pltpu.make_async_copy(tb.at[G], tb.at[G], recv_t.at[G]).wait()

    for k in range(1, G):
        s = flipped(g, k)
        pltpu.make_async_copy(tb.at[s], tb.at[s], recv_t.at[s]).wait()

    def build(d, carry):
        pair = jnp.concatenate([tb[d], tb[d + 1]], axis=1)
        ut[d, 0:Q * JS, :] = tb[d]
        for s in range(1, TAUS // Q):
            ut[d, s * Q * JS:(s + 1) * Q * JS, :] = pair[:, s:s + R]
        return carry

    lax.fori_loop(0, G, build, 0)

    def multiply(d, first):
        weights = vbuf[d].reshape(Q // 2 * R, 256)

        def tile(i, carry):
            r0 = pl.multiple_of(i * TILE, JS)
            left = jnp.concatenate(
                [ut[d, pl.ds(pl.multiple_of(r0 + 2 * JS * e, JS), TILE), :] for e in range(Q // 2)], axis=1)
            part = jnp.dot(left, weights, preferred_element_type=jnp.float32)
            for h in range(2):
                half = part[:, h * 128:(h + 1) * 128]
                if first:
                    acc[h, pl.ds(r0, TILE), :] = half
                else:
                    acc[h, pl.ds(r0, TILE), :] += half
            return carry

        lax.fori_loop(0, OUT_ROWS // TILE, tile, 0)

    def wait_v(s, h):
        part = vbuf.at[s, pl.ds(h * half, half)]
        pltpu.make_async_copy(part, part, recv_v.at[s, h]).wait()

    def wait_both(s):
        wait_v(s, 0)
        wait_v(s, 1)

    multiply(g, True)
    wait_both(partner)
    multiply(partner, False)
    if relay:
        x, y, z = (flipped(g, mask) for mask in (2, 4, 6))
        wait_v(x, 1)
        send(x, y, 1, 3)
        wait_v(y, 0)
        send(y, x, 0, 3)
        send(x, partner, 1, 4)
        send(y, partner, 0, 5)
        wait_v(x, 0)
        send(x, partner, 0, 4)
        wait_v(y, 1)
        send(y, partner, 1, 5)
        multiply(x, False)
        multiply(y, False)
        for mask in (3, 5):
            wait_both(flipped(g, mask))
            multiply(flipped(g, mask), False)
        for h in range(2):
            wait_v(z, h)
            send(z, partner, h, 6)
        multiply(z, False)
        wait_both(flipped(g, 7))
        multiply(flipped(g, 7), False)
    else:
        for c in range(1, C):
            s = flipped(g, 2 * c)
            for h in range(2):
                wait_v(s, h)
                send(s, partner, h, C + c - 1)
            multiply(s, False)
            if c > 1:
                s2 = flipped(g, 2 * (c - 1) + 1)
                wait_both(s2)
                multiply(s2, False)
        if C > 1:
            s2 = flipped(g, 2 * (C - 1) + 1)
            wait_both(s2)
            multiply(s2, False)

    def piece(j):
        full = acc[0, pl.ds(j, LAGS, stride=JS), :] + acc[1, pl.ds(JS + j, LAGS, stride=JS), :]
        if iw == 128:
            return full
        return sum(jnp.where(g % (128 // iw) == h, full[:, h * iw:(h + 1) * iw], 0.0) for h in range(128 // iw))

    def copy_r(k):
        d = (t + k) % T
        return pltpu.make_async_remote_copy(
            src_ref=sbuf.at[d], dst_ref=rbuf.at[t], send_sem=send_r.at[k], recv_sem=recv_r.at[t],
            device_id=(d * G + g,), device_id_type=MESH)

    for k in list(range(1, T)) + [0]:
        d = (t + k) % T
        for m in range(mj):
            if k:
                sbuf[d, m] = encoded(piece(d * mj + m), m_code, levels)
            else:
                out[:, m * iw:(m + 1) * iw] = piece(d * mj + m)
        if k:
            copy_r(k).start()
    for k in range(1, T):
        s = (t + T - k) % T
        pltpu.make_async_copy(rbuf.at[s], rbuf.at[s], recv_r.at[s]).wait()
        for m in range(mj):
            out[:, m * iw:(m + 1) * iw] += decoded(rbuf[s, m], m_code, levels)

    for k in range(1, G):
        copy_t(k).wait_send()

    @pl.when(jnp.logical_and(g == 0, t > 0))
    def _():
        for d in range(G):
            copy_h(d).wait_send()

    for what in sends:
        copy_v(*what).wait_send()
    for k in range(1, T):
        copy_r(k).wait_send()


def on_device(n, samples):
    rows, width = samples.shape
    owned = width * width // n
    mj = max(1, owned // width)
    iw = min(width, owned)
    T = JS // mj
    G = n // T
    R = rows // Q
    perm = np.zeros((G * JS, width), np.float32)
    for d in range(G):
        for s in range(T):
            for m in range(mj):
                perm[d * JS + s * mj + m, (s * G + d) * owned // width + m] = 1
    lagged = pl.pallas_call(
        functools.partial(kernel, n, T, G, mj, iw),
        out_shape=jax.ShapeDtypeStruct((LAGS, owned), jnp.float32),
        in_specs=[pl.BlockSpec(memory_space=pltpu.VMEM)] * 2,
        out_specs=pl.BlockSpec(memory_space=pltpu.VMEM),
        scratch_shapes=[
            pltpu.VMEM((G, Q // 2, R, 2 * width), jnp.bfloat16),
            pltpu.VMEM((G, Q * JS, R), jnp.bfloat16),
            pltpu.VMEM((G + 1, Q * JS, R), jnp.bfloat16),
            pltpu.VMEM((G, TAUS * JS, R), jnp.bfloat16),
            pltpu.VMEM((2, OUT_ROWS, width), jnp.float32),
            pltpu.VMEM((T, mj, LAGS, iw), jnp.int16),
            pltpu.VMEM((T, mj, LAGS, iw), jnp.int16),
            pltpu.SemaphoreType.DMA((G, 2)),
            pltpu.SemaphoreType.DMA((G, 2)),
            pltpu.SemaphoreType.DMA((G,)),
            pltpu.SemaphoreType.DMA((G + 1,)),
            pltpu.SemaphoreType.DMA((G,)),
            pltpu.SemaphoreType.DMA((T,)),
            pltpu.SemaphoreType.DMA((T,)),
        ],
        compiler_params=pltpu.CompilerParams(has_side_effects=True, collective_id=0, vmem_limit_bytes=56 * 1024 * 1024),
    )(samples, jnp.asarray(perm, jnp.bfloat16))
    k = np.arange(LAGS)
    angle = 2.0 * np.pi / LAGS * (np.outer(k, k) % LAGS)
    table = np.concatenate([np.cos(angle), -np.sin(angle)]) / (16.0 * rows * n)
    spectra = jnp.dot(
        jnp.asarray(table, jnp.float32), lagged,
        preferred_element_type=jnp.float32, precision=lax.Precision.HIGH)
    return spectra.reshape(2, LAGS, owned)


def solution(mesh):
    return jax.shard_map(
        functools.partial(on_device, mesh.shape["tm"]), mesh=mesh,
        in_specs=(P("tm", None),), out_specs=P(None, None, "tm"), check_vma=False)
```

profile of v0, /device:TPU:0, one launch (start us, length us, event | category | flops | bytes accessed | tf_op | source)
XLA Modules:
  0.0 52.2 jit_solution(11530093996007899473)
XLA Ops:
  0.0 0.0 copy-start
  0.0 50.1 %shard_map.37 = f32[128,512]{1,0:T(8,128)} custom-call(s32[2048,128]{1,0:T(8,128)} %samples.1, bf16[128,128]{1,0:T(8,128)(2,1)} %constant.4.clone.perm), custom_call_target="tpu_custom_call" | custom-call | tf_op jit(solution)/shard_map/pallas_call | solution.py:289
  50.1 0.0 copy-done
  50.1 2.1 %fusion = f32[256,512]{1,0:T(8,128)} fusion(f32[256,128]{1,0:T(8,128)S(1)} %copy-done, f32[128,512]{1,0:T(8,128)} %shard_map.37), kind=kOutput, calls=%fused_computation | convolution fusion | flops 100663296 | bytes 917504 | tf_op jit(solution)/shard_map/dot_general | solution.py:315
Async XLA Ops:
  0.0 50.1 %copy-start = (f32[256,128]{1,0:T(8,128)S(1)}, f32[256,128]{1,0:T(8,128)}, u32[]{:S(2)}) copy-start(f32[256,128]{1,0:T(8,128)} %constant.5.clone) | copy-start | bytes 393220
where the time goes:
time: 53 us; the launch traced here: 52.2 us
  Pallas kernels  50.1 us (95%)
  matrix products  2.11 us (4%)
    pallas_call x1, Pallas kernels, on_device(): pl.pallas_call(functools.partial(kernel, n, T, G, mj, iw), out_shape=jax....  50.1 us
    dot_general x1, matrix products, on_device(): jnp.dot(jnp.asarray(table, jnp.float32), lagged, preferred_element_type=j...  2.11 us

commit v1 on v0

--- a/solution.py
+++ b/solution.py
@@ -14,6 +14,7 @@
 TAUS = LAGS + Q
 OUT_ROWS = (LAGS + 1) * JS
 TILE = OUT_ROWS // 3
+CHUNKS = 4
 MESH = pl.DeviceIdType.MESH
 
 
@@ -273,7 +274,290 @@
         copy_r(k).wait_send()
 
 
-def on_device(n, samples):
+def other(index, mask):
+    out = index
+    bit = 1
+    while bit <= mask:
+        if mask & bit:
+            out = out + bit - 2 * bit * ((index // bit) % 2)
+        bit *= 2
+    return out
+
+
+def unit(limit):
+    step = -(-limit // 32000)
+    return step, 32700 // step
+
+
+def shrunk(x, limit, axis=0):
+    step, levels = unit(limit)
+    largest = jnp.max(jnp.abs(x), axis=axis)
+    scale = (largest * (1.0 / step)).astype(jnp.int32) + 1
+    return scale.astype(jnp.int16), float(levels) / scale.astype(jnp.float32)
+
+
+def whole(code):
+    return code.astype(jnp.int32).astype(jnp.float32)
+
+
+def chip_kernel(n, mj, samples, perm, out, vbuf, ts, tb, ut, acc, hs, hr, su, ru, sz, rz, sc,
+                send_v, recv_v, send_h, recv_h, send_u, recv_u, send_z, recv_z):
+    me = lax.axis_index("tm")
+    core = me % 2
+    chip = me // 2
+    x = chip % 2
+    y = (chip // 2) % 2
+    z = chip // 4
+    chips = n // 2
+    Z = chips // 4
+    rows = samples.shape[0]
+    R = rows // Q
+    L = LAGS // CHUNKS
+    half = L * JS // 2
+    HL = L // 2
+    limits = [2 * rows * 64 * s for s in (1, 2, 4)]
+    reach = TAUS // Q
+
+    barrier = pltpu.get_barrier_semaphore()
+
+    def greet(device):
+        pl.semaphore_signal(barrier, inc=1, device_id=(device,), device_id_type=MESH)
+
+    along_x = other(me, 2)
+    along_y = other(me, 4)
+    partner = other(me, 1)
+    for device in (partner, along_x, along_y):
+        greet(device)
+    for k in range(1, Z):
+        greet((z + k) % Z * 8 + me % 8)
+
+    @pl.when(chip < chips - 1)
+    def _():
+        greet(2 * chip + 2)
+
+    leads = jnp.logical_and(core == 0, chip > 0)
+
+    for q in range(0, Q, 2):
+        pair = [samples[pl.ds(q + p, reach - 1, stride=Q), :].astype(jnp.float32) for p in range(2)]
+        hs[q * (reach - 1):(q + 2) * (reach - 1), :] = jnp.concatenate(pair, axis=0).astype(jnp.bfloat16)
+    for q in range(Q):
+        phase = samples[pl.ds(q, R, stride=Q), :].astype(jnp.float32).astype(jnp.bfloat16)
+        vbuf[core, q // 2, :, (q % 2) * 128:(q % 2 + 1) * 128] = phase
+
+    pl.semaphore_wait(barrier, jnp.where(leads, 4 + Z, 2 + Z))
+
+    def copy_h(k):
+        return pltpu.make_async_remote_copy(
+            src_ref=hs, dst_ref=hr, send_sem=send_h.at[k], recv_sem=recv_h.at[0],
+            device_id=(2 * chip - 2 + k,), device_id_type=MESH)
+
+    @pl.when(leads)
+    def _():
+        for k in range(2):
+            copy_h(k).start()
+
+    def copy_v(k):
+        src, dst = ((vbuf.at[core], vbuf.at[core]), (ts.at[1 - core], tb.at[core]))[k]
+        return pltpu.make_async_remote_copy(
+            src_ref=src, dst_ref=dst, send_sem=send_v.at[k], recv_sem=recv_v.at[k],
+            device_id=(partner,), device_id_type=MESH)
+
+    copy_v(0).start()
+
+    def transposed(block):
+        return lax.dot_general(perm[...], block, (((1,), (1,)), ((), ())), preferred_element_type=jnp.float32)
+
+    for q in range(Q):
+        turned = transposed(vbuf[core, q // 2, :, (q % 2) * 128:(q % 2 + 1) * 128]).astype(jnp.bfloat16)
+        for k in range(2):
+            for a in range(4):
+                r0 = (k * 4 + a) * JS
+                ts[k, a, q * JS:(q + 1) * JS, :] = turned[r0:r0 + JS, :]
+
+    copy_v(1).start()
+    tb[core] = ts[core]
+
+    @pl.when(chip == chips - 1)
+    def _():
+        hr[...] = jnp.zeros(hr.shape, hr.dtype)
+
+    @pl.when(chip < chips - 1)
+    def _():
+        pltpu.make_async_copy(hr, hr, recv_h.at[0]).wait()
+
+    edge = lax.dot_general(
+        perm[pl.ds(pl.multiple_of(core * 4 * JS, 4 * JS), 4 * JS), :], hr[...],
+        (((1,), (1,)), ((), ())), preferred_element_type=jnp.float32)
+    for q in range(Q):
+        moved = edge if q == 0 else pltpu.roll(edge, 128 - q * (reach - 1), 1)
+        for a in range(4):
+            tb[2, a, q * JS:(q + 1) * JS, :] = moved[a * JS:(a + 1) * JS, :].astype(jnp.bfloat16)
+
+    for k in range(2):
+        there = (vbuf, tb)[k].at[1 - core]
+        pltpu.make_async_copy(there, there, recv_v.at[k]).wait()
+
+    def build(first, last):
+        def one(a, carry):
+            for d in range(2):
+                pair = jnp.concatenate([tb[d, a], tb[d + 1, a]], axis=1)
+                for s in range(first, last):
+                    ut[a, d, s * Q * JS:(s + 1) * Q * JS, :] = pair[:, s:s + R]
+            return carry
+
+        lax.fori_loop(0, 4, one, 0)
+
+    def copy_u(t, k):
+        return pltpu.make_async_remote_copy(
+            src_ref=su.at[t, k], dst_ref=ru.at[t, k], send_sem=send_u.at[t, k], recv_sem=recv_u.at[t, k],
+            device_id=(along_x if k in (0, 1, 5) else along_y,), device_id_type=MESH)
+
+    def send(t, k, values, limit):
+        blocks = values.reshape(HL, JS, 128)
+        code, scale = shrunk(blocks, limit)
+        su[t, k, 0:half, :] = jnp.round(blocks * scale[None]).reshape(half, 128).astype(jnp.int32).astype(jnp.int16)
+        su[t, k, half:half + JS, :] = code
+        copy_u(t, k).start()
+
+    def received(t, k, limit):
+        pltpu.make_async_copy(ru.at[t, k], ru.at[t, k], recv_u.at[t, k]).wait()
+        scale = whole(ru[t, k, half:half + JS, :]) * (1.0 / unit(limit)[1])
+        blocks = whole(ru[t, k, 0:half, :]).reshape(HL, JS, 128)
+        return (blocks * scale[None]).reshape(half, 128)
+
+    def multiply(q, t):
+        a = (x, 1 - x)[q % 2] + 2 * (y, 1 - y)[q // 2]
+        r0 = t * L * JS
+        tall = (L + 1) * JS
+        left = jnp.concatenate(
+            [ut[a, d, r0 + 2 * JS * e:r0 + 2 * JS * e + tall, :] for d in range(2) for e in range(Q // 2)], axis=1)
+        part = jnp.dot(left, vbuf[...].reshape(Q * R, 256), preferred_element_type=jnp.float32)
+        full = part[0:L * JS, 0:128] + part[JS:tall, 128:256]
+        if q == 3:
+            send(t, 0, full[0:half], limits[0])
+            send(t, 2, full[half:], limits[0])
+        elif q == 1:
+            send(t, 1, full[0:half], limits[0])
+            acc[q, r0 + half:r0 + 2 * half, :] = full[half:]
+        elif q == 2:
+            send(t, 3, full[half:], limits[0])
+            acc[q, r0:r0 + half, :] = full[0:half]
+        else:
+            acc[q, r0:r0 + 2 * half, :] = full
+
+    def second(t):
+        r0 = t * L * JS
+        send(t, 4, acc[2, r0:r0 + half, :] + received(t, 0, limits[0]), limits[1])
+        send(t, 5, acc[1, r0 + half:r0 + 2 * half, :] + received(t, 2, limits[0]), limits[1])
+
+    def copy_z(t, k):
+        d = (z + k) % Z
+        return pltpu.make_async_remote_copy(
+            src_ref=sz.at[d, t], dst_ref=rz.at[z, t], send_sem=send_z.at[k, t], recv_sem=recv_z.at[z, t],
+            device_id=(d * 8 + me % 8,), device_id_type=MESH)
+
+    def third(t):
+        r0 = t * L * JS
+        for h in range(2):
+            near, far = ((1, 4), (3, 5))[h]
+            acc[0, r0 + h * half:r0 + (h + 1) * half, :] += received(t, near, limits[0]) + received(t, far, limits[1])
+        code, scale = shrunk(acc[0, r0:r0 + 2 * half, :].reshape(L, JS, 128), limits[2])
+        sc[t, 0] = scale
+        for k in range(1, Z):
+            d = (z + k) % Z
+            for m in range(mj):
+                j = d * mj + m
+                values = acc[0, pl.ds(r0 + j, L, stride=JS), :] * sc[t, 0, pl.ds(j, 1), :]
+                sz[d, t, m * L:(m + 1) * L, :] = jnp.round(values).astype(jnp.int32).astype(jnp.int16)
+            sz[d, t, mj * L:mj * L + JS, :] = code
+            copy_z(t, k).start()
+        for m in range(mj):
+            out[t * L:(t + 1) * L, m * 128:(m + 1) * 128] = acc[0, pl.ds(r0 + z * mj + m, L, stride=JS), :]
+
+    def fourth(t):
+        for k in range(1, Z):
+            s = (z + Z - k) % Z
+            pltpu.make_async_copy(rz.at[s, t], rz.at[s, t], recv_z.at[s, t]).wait()
+            sc[t, k] = whole(rz[s, t, mj * L:mj * L + JS, :]) * (1.0 / unit(limits[2])[1])
+            for m in range(mj):
+                out[t * L:(t + 1) * L, m * 128:(m + 1) * 128] += (
+                    whole(rz[s, t, m * L:(m + 1) * L, :]) * sc[t, k, pl.ds(z * mj + m, 1), :])
+
+    grown = 0
+    for t in range(CHUNKS + 2):
+        if t < CHUNKS:
+            need = -(-((t + 1) * L + Q - 1) // Q)
+            build(grown, need)
+            grown = need
+            for q in (3, 1, 2, 0):
+                multiply(q, t)
+        if 0 <= t - 1 < CHUNKS:
+            second(t - 1)
+        if 0 <= t - 2 < CHUNKS:
+            third(t - 2)
+    for t in range(CHUNKS):
+        fourth(t)
+
+    @pl.when(leads)
+    def _():
+        for k in range(2):
+            copy_h(k).wait_send()
+
+    for k in range(2):
+        copy_v(k).wait_send()
+    for t in range(CHUNKS):
+        for k in range(6):
+            copy_u(t, k).wait_send()
+        for k in range(1, Z):
+            copy_z(t, k).wait_send()
+
+
+def chip_lags(n, samples):
+    rows, width = samples.shape
+    owned = width * width // n
+    mj = owned // width
+    Z = n // 8
+    R = rows // Q
+    L = LAGS // CHUNKS
+    perm = np.zeros((width, width), np.float32)
+    for core in range(2):
+        for a in range(4):
+            for d in range(Z):
+                for m in range(mj):
+                    perm[(core * 4 + a) * JS + d * mj + m, (d * 8 + a * 2 + core) * mj + m] = 1
+    tall = L * JS // 2 + JS
+    return pl.pallas_call(
+        functools.partial(chip_kernel, n, mj),
+        out_shape=jax.ShapeDtypeStruct((LAGS, owned), jnp.float32),
+        in_specs=[pl.BlockSpec(memory_space=pltpu.VMEM)] * 2,
+        out_specs=pl.BlockSpec(memory_space=pltpu.VMEM),
+        scratch_shapes=[
+            pltpu.VMEM((2, Q // 2, R, 2 * width), jnp.bfloat16),
+            pltpu.VMEM((2, 4, Q * JS, R), jnp.bfloat16),
+            pltpu.VMEM((3, 4, Q * JS, R), jnp.bfloat16),
+            pltpu.VMEM((4, 2, TAUS * JS, R), jnp.bfloat16),
+            pltpu.VMEM((3, LAGS * JS, width), jnp.float32),
+            pltpu.VMEM((Q * (TAUS // Q - 1), width), jnp.bfloat16),
+            pltpu.VMEM((Q * (TAUS // Q - 1), width), jnp.bfloat16),
+            pltpu.VMEM((CHUNKS, 6, tall, width), jnp.int16),
+            pltpu.VMEM((CHUNKS, 6, tall, width), jnp.int16),
+            pltpu.VMEM((Z, CHUNKS, mj * L + JS, width), jnp.int16),
+            pltpu.VMEM((Z, CHUNKS, mj * L + JS, width), jnp.int16),
+            pltpu.VMEM((CHUNKS, Z, JS, width), jnp.float32),
+            pltpu.SemaphoreType.DMA((2,)),
+            pltpu.SemaphoreType.DMA((2,)),
+            pltpu.SemaphoreType.DMA((2,)),
+            pltpu.SemaphoreType.DMA((1,)),
+            pltpu.SemaphoreType.DMA((CHUNKS, 6)),
+            pltpu.SemaphoreType.DMA((CHUNKS, 6)),
+            pltpu.SemaphoreType.DMA((Z, CHUNKS)),
+            pltpu.SemaphoreType.DMA((Z, CHUNKS)),
+        ],
+        compiler_params=pltpu.CompilerParams(has_side_effects=True, collective_id=1, vmem_limit_bytes=56 * 1024 * 1024),
+    )(samples, jnp.asarray(perm, jnp.bfloat16))
+
+
+def gathered_lags(n, samples):
     rows, width = samples.shape
     owned = width * width // n
     mj = max(1, owned // width)
@@ -286,7 +570,7 @@
         for s in range(T):
             for m in range(mj):
                 perm[d * JS + s * mj + m, (s * G + d) * owned // width + m] = 1
-    lagged = pl.pallas_call(
+    return pl.pallas_call(
         functools.partial(kernel, n, T, G, mj, iw),
         out_shape=jax.ShapeDtypeStruct((LAGS, owned), jnp.float32),
         in_specs=[pl.BlockSpec(memory_space=pltpu.VMEM)] * 2,
@@ -309,6 +593,13 @@
         ],
         compiler_params=pltpu.CompilerParams(has_side_effects=True, collective_id=0, vmem_limit_bytes=56 * 1024 * 1024),
     )(samples, jnp.asarray(perm, jnp.bfloat16))
+
+
+def on_device(n, samples):
+    rows, width = samples.shape
+    owned = width * width // n
+    lags = chip_lags if owned >= width and n % 8 == 0 else gathered_lags
+    lagged = lags(n, samples)
     k = np.arange(LAGS)
     angle = 2.0 * np.pi / LAGS * (np.outer(k, k) % LAGS)
     table = np.concatenate([np.cos(angle), -np.sin(angle)]) / (16.0 * rows * n)

time: 53 us -> 49.3 us (0.930); the launches traced: 52.2 us -> 49.2 us
  Pallas kernels: 50.1 us -> 47 us
    pallas_call x1, Pallas kernels: 50.1 us -> 47 us  [chip_lags(): pl.pallas_call(functools.partial(chip_kernel, n, mj), out_shape=jax.Shape...]
where the time goes in v1:
time: 49.3 us; the launch traced here: 49.2 us
  Pallas kernels  47 us (95%)
  matrix products  2.11 us (4%)
    pallas_call x1, Pallas kernels, chip_lags(): pl.pallas_call(functools.partial(chip_kernel, n, mj), out_shape=jax.Shape...  47 us
    dot_general x1, matrix products, on_device(): jnp.dot(jnp.asarray(table, jnp.float32), lagged, preferred_element_type=j...  2.11 us

profile of v1, /device:TPU:0, one launch (start us, length us, event | category | flops | bytes accessed | tf_op | source)
XLA Modules:
  0.0 49.2 jit_solution(7062497812787465159)
XLA Ops:
  0.0 0.0 copy-start
  0.0 47.0 %shard_map.37 = f32[128,512]{1,0:T(8,128)} custom-call(s32[2048,128]{1,0:T(8,128)} %samples.1, bf16[128,128]{1,0:T(8,128)(2,1)} %constant.4.clone.perm), custom_call_target="tpu_custom_call" | custom-call | tf_op jit(solution)/shard_map/pallas_call | solution.py:529
  47.1 0.0 copy-done
  47.1 2.1 %fusion = f32[256,512]{1,0:T(8,128)} fusion(f32[256,128]{1,0:T(8,128)S(1)} %copy-done, f32[128,512]{1,0:T(8,128)} %shard_map.37), kind=kOutput, calls=%fused_computation | convolution fusion | flops 100663296 | bytes 917504 | tf_op jit(solution)/shard_map/dot_general | solution.py:606
Async XLA Ops:
  0.0 47.1 %copy-start = (f32[256,128]{1,0:T(8,128)S(1)}, f32[256,128]{1,0:T(8,128)}, u32[]{:S(2)}) copy-start(f32[256,128]{1,0:T(8,128)} %constant.5.clone) | copy-start | bytes 393220

commit v2 on v1

--- a/solution.py
+++ b/solution.py
@@ -14,7 +14,7 @@
 TAUS = LAGS + Q
 OUT_ROWS = (LAGS + 1) * JS
 TILE = OUT_ROWS // 3
-CHUNKS = 4
+CHUNKS = (32, 32, 32, 16, 16)
 MESH = pl.DeviceIdType.MESH
 
 
@@ -300,8 +300,8 @@
     return code.astype(jnp.int32).astype(jnp.float32)
 
 
-def chip_kernel(n, mj, samples, perm, out, vbuf, ts, tb, ut, acc, hs, hr, su, ru, sz, rz, sc,
-                send_v, recv_v, send_h, recv_h, send_u, recv_u, send_z, recv_z):
+def chip_kernel(n, mj, samples, perm, out, sv, vbuf, ts, tb, ut, acc, hs, hr, su, ru, sz, rz, sc,
+                load, heard, send_v, recv_v, send_h, recv_h, send_u, recv_u, send_z, recv_z):
     me = lax.axis_index("tm")
     core = me % 2
     chip = me // 2
@@ -312,9 +312,8 @@
     Z = chips // 4
     rows = samples.shape[0]
     R = rows // Q
-    L = LAGS // CHUNKS
-    half = L * JS // 2
-    HL = L // 2
+    starts = [sum(CHUNKS[:t]) for t in range(len(CHUNKS))]
+    rounds = max(2, Z - 2)
     limits = [2 * rows * 64 * s for s in (1, 2, 4)]
     reach = TAUS // Q
 
@@ -326,43 +325,48 @@
     along_x = other(me, 2)
     along_y = other(me, 4)
     partner = other(me, 1)
-    for device in (partner, along_x, along_y):
-        greet(device)
-    for k in range(1, Z):
-        greet((z + k) % Z * 8 + me % 8)
-
-    @pl.when(chip < chips - 1)
-    def _():
-        greet(2 * chip + 2)
-
-    leads = jnp.logical_and(core == 0, chip > 0)
+    up = me + 8
+    down = me - 8
+
+    def near(tell):
+        tell(along_x)
+        tell(along_y)
+        pl.when(z > 0)(lambda: tell(down))
+        pl.when(z < Z - 1)(lambda: tell(up))
+
+    around = 2 + jnp.where(z > 0, 1, 0) + jnp.where(z < Z - 1, 1, 0)
+    greet(partner)
+    near(greet)
+    fetch = pltpu.make_async_copy(samples, sv, load.at[0])
+    fetch.start()
+    fetch.wait()
 
     for q in range(0, Q, 2):
-        pair = [samples[pl.ds(q + p, reach - 1, stride=Q), :].astype(jnp.float32) for p in range(2)]
-        hs[q * (reach - 1):(q + 2) * (reach - 1), :] = jnp.concatenate(pair, axis=0).astype(jnp.bfloat16)
+        pair = [sv[pl.ds(q + p, reach - 1, stride=Q), :].astype(jnp.float32) for p in range(2)]
+        hs[0, q * (reach - 1):(q + 2) * (reach - 1), :] = jnp.concatenate(pair, axis=0).astype(jnp.bfloat16)
     for q in range(Q):
-        phase = samples[pl.ds(q, R, stride=Q), :].astype(jnp.float32).astype(jnp.bfloat16)
+        phase = sv[pl.ds(q, R, stride=Q), :].astype(jnp.float32).astype(jnp.bfloat16)
         vbuf[core, q // 2, :, (q % 2) * 128:(q % 2 + 1) * 128] = phase
 
-    pl.semaphore_wait(barrier, jnp.where(leads, 4 + Z, 2 + Z))
-
-    def copy_h(k):
-        return pltpu.make_async_remote_copy(
-            src_ref=hs, dst_ref=hr, send_sem=send_h.at[k], recv_sem=recv_h.at[0],
-            device_id=(2 * chip - 2 + k,), device_id_type=MESH)
-
-    @pl.when(leads)
-    def _():
-        for k in range(2):
-            copy_h(k).start()
+    pl.semaphore_wait(barrier, around + 1)
+
+    def tell(stage):
+        near(lambda device: pl.semaphore_signal(
+            heard.at[stage], inc=1, device_id=(device,), device_id_type=MESH))
+
+    tell(0)
 
     def copy_v(k):
-        src, dst = ((vbuf.at[core], vbuf.at[core]), (ts.at[1 - core], tb.at[core]))[k]
+        src, dst = ((hs.at[0], hs.at[1]), (vbuf.at[core], vbuf.at[core]), (ts.at[1 - core], tb.at[core]))[k]
         return pltpu.make_async_remote_copy(
             src_ref=src, dst_ref=dst, send_sem=send_v.at[k], recv_sem=recv_v.at[k],
             device_id=(partner,), device_id_type=MESH)
 
-    copy_v(0).start()
+    @pl.when(core == 0)
+    def _():
+        copy_v(0).start()
+
+    copy_v(1).start()
 
     def transposed(block):
         return lax.dot_general(perm[...], block, (((1,), (1,)), ((), ())), preferred_element_type=jnp.float32)
@@ -374,8 +378,25 @@
                 r0 = (k * 4 + a) * JS
                 ts[k, a, q * JS:(q + 1) * JS, :] = turned[r0:r0 + JS, :]
 
-    copy_v(1).start()
+    copy_v(2).start()
     tb[core] = ts[core]
+
+    @pl.when(core == 1)
+    def _():
+        pltpu.make_async_copy(hs.at[1], hs.at[1], recv_v.at[0]).wait()
+
+    def copy_h(k):
+        return pltpu.make_async_remote_copy(
+            src_ref=hs.at[k], dst_ref=hr, send_sem=send_h.at[k], recv_sem=recv_h.at[0],
+            device_id=(me - 2,), device_id_type=MESH)
+
+    for stage in range(rounds):
+        pl.semaphore_wait(heard.at[stage], around)
+        if stage < rounds - 1:
+            tell(stage + 1)
+
+    for k in range(2):
+        pl.when(jnp.logical_and(chip > 0, core == k))(copy_h(k).start)
 
     @pl.when(chip == chips - 1)
     def _():
@@ -395,7 +416,7 @@
 
     for k in range(2):
         there = (vbuf, tb)[k].at[1 - core]
-        pltpu.make_async_copy(there, there, recv_v.at[k]).wait()
+        pltpu.make_async_copy(there, there, recv_v.at[k + 1]).wait()
 
     def build(first, last):
         def one(a, carry):
@@ -408,104 +429,116 @@
         lax.fori_loop(0, 4, one, 0)
 
     def copy_u(t, k):
-        return pltpu.make_async_remote_copy(
-            src_ref=su.at[t, k], dst_ref=ru.at[t, k], send_sem=send_u.at[t, k], recv_sem=recv_u.at[t, k],
+        rows_u = pl.ds(0, (CHUNKS[t] // 2 + 1) * JS)
+        return pltpu.make_async_remote_copy(
+            src_ref=su.at[t, k, rows_u], dst_ref=ru.at[t, k, rows_u],
+            send_sem=send_u.at[t, k], recv_sem=recv_u.at[t, k],
             device_id=(along_x if k in (0, 1, 5) else along_y,), device_id_type=MESH)
 
     def send(t, k, values, limit):
-        blocks = values.reshape(HL, JS, 128)
+        half = CHUNKS[t] * JS // 2
+        blocks = values.reshape(CHUNKS[t] // 2, JS, 128)
         code, scale = shrunk(blocks, limit)
         su[t, k, 0:half, :] = jnp.round(blocks * scale[None]).reshape(half, 128).astype(jnp.int32).astype(jnp.int16)
         su[t, k, half:half + JS, :] = code
         copy_u(t, k).start()
 
     def received(t, k, limit):
-        pltpu.make_async_copy(ru.at[t, k], ru.at[t, k], recv_u.at[t, k]).wait()
+        half = CHUNKS[t] * JS // 2
+        here = ru.at[t, k, pl.ds(0, half + JS)]
+        pltpu.make_async_copy(here, here, recv_u.at[t, k]).wait()
         scale = whole(ru[t, k, half:half + JS, :]) * (1.0 / unit(limit)[1])
-        blocks = whole(ru[t, k, 0:half, :]).reshape(HL, JS, 128)
+        blocks = whole(ru[t, k, 0:half, :]).reshape(CHUNKS[t] // 2, JS, 128)
         return (blocks * scale[None]).reshape(half, 128)
+
+    def rows_of(t, h):
+        half = CHUNKS[t] * JS // 2
+        return starts[t] * JS + h * half, half
 
     def multiply(q, t):
         a = (x, 1 - x)[q % 2] + 2 * (y, 1 - y)[q // 2]
-        r0 = t * L * JS
-        tall = (L + 1) * JS
-        left = jnp.concatenate(
-            [ut[a, d, r0 + 2 * JS * e:r0 + 2 * JS * e + tall, :] for d in range(2) for e in range(Q // 2)], axis=1)
-        part = jnp.dot(left, vbuf[...].reshape(Q * R, 256), preferred_element_type=jnp.float32)
-        full = part[0:L * JS, 0:128] + part[JS:tall, 128:256]
-        if q == 3:
-            send(t, 0, full[0:half], limits[0])
-            send(t, 2, full[half:], limits[0])
-        elif q == 1:
-            send(t, 1, full[0:half], limits[0])
-            acc[q, r0 + half:r0 + 2 * half, :] = full[half:]
-        elif q == 2:
-            send(t, 3, full[half:], limits[0])
-            acc[q, r0:r0 + half, :] = full[0:half]
-        else:
-            acc[q, r0:r0 + 2 * half, :] = full
+        full = []
+        for h in range(2):
+            r0, half = rows_of(t, h)
+            left = jnp.concatenate(
+                [ut[a, d, r0 + 2 * JS * e:r0 + 2 * JS * e + half + JS, :] for d in range(2) for e in range(Q // 2)], axis=1)
+            part = jnp.dot(left, vbuf[...].reshape(Q * R, 256), preferred_element_type=jnp.float32)
+            full.append(part[0:half, 0:128] + part[JS:half + JS, 128:256])
+        for h in range(2):
+            r0, half = rows_of(t, h)
+            if q == 3 or q == h + 1:
+                send(t, 2 * h + (0 if q == 3 else 1), full[h], limits[0])
+            else:
+                acc[q, r0:r0 + half, :] = full[h]
 
     def second(t):
-        r0 = t * L * JS
-        send(t, 4, acc[2, r0:r0 + half, :] + received(t, 0, limits[0]), limits[1])
-        send(t, 5, acc[1, r0 + half:r0 + 2 * half, :] + received(t, 2, limits[0]), limits[1])
+        for h in range(2):
+            r0, half = rows_of(t, h)
+            send(t, 4 + h, acc[2 - h, r0:r0 + half, :] + received(t, 2 * h, limits[0]), limits[1])
 
     def copy_z(t, k):
         d = (z + k) % Z
-        return pltpu.make_async_remote_copy(
-            src_ref=sz.at[d, t], dst_ref=rz.at[z, t], send_sem=send_z.at[k, t], recv_sem=recv_z.at[z, t],
+        rows_z = pl.ds(0, mj * CHUNKS[t] + JS)
+        return pltpu.make_async_remote_copy(
+            src_ref=sz.at[d, t, rows_z], dst_ref=rz.at[z, t, rows_z],
+            send_sem=send_z.at[k, t], recv_sem=recv_z.at[z, t],
             device_id=(d * 8 + me % 8,), device_id_type=MESH)
 
     def third(t):
-        r0 = t * L * JS
+        L = CHUNKS[t]
+        first = starts[t] * JS
         for h in range(2):
-            near, far = ((1, 4), (3, 5))[h]
-            acc[0, r0 + h * half:r0 + (h + 1) * half, :] += received(t, near, limits[0]) + received(t, far, limits[1])
-        code, scale = shrunk(acc[0, r0:r0 + 2 * half, :].reshape(L, JS, 128), limits[2])
+            r0, half = rows_of(t, h)
+            acc[0, r0:r0 + half, :] += received(t, 2 * h + 1, limits[0]) + received(t, 4 + h, limits[1])
+        code, scale = shrunk(acc[0, first:first + L * JS, :].reshape(L, JS, 128), limits[2])
         sc[t, 0] = scale
         for k in range(1, Z):
             d = (z + k) % Z
             for m in range(mj):
                 j = d * mj + m
-                values = acc[0, pl.ds(r0 + j, L, stride=JS), :] * sc[t, 0, pl.ds(j, 1), :]
+                values = acc[0, pl.ds(first + j, L, stride=JS), :] * sc[t, 0, pl.ds(j, 1), :]
                 sz[d, t, m * L:(m + 1) * L, :] = jnp.round(values).astype(jnp.int32).astype(jnp.int16)
             sz[d, t, mj * L:mj * L + JS, :] = code
             copy_z(t, k).start()
         for m in range(mj):
-            out[t * L:(t + 1) * L, m * 128:(m + 1) * 128] = acc[0, pl.ds(r0 + z * mj + m, L, stride=JS), :]
+            out[starts[t]:starts[t] + L, m * 128:(m + 1) * 128] = acc[0, pl.ds(first + z * mj + m, L, stride=JS), :]
 
     def fourth(t):
+        L = CHUNKS[t]
         for k in range(1, Z):
             s = (z + Z - k) % Z
-            pltpu.make_async_copy(rz.at[s, t], rz.at[s, t], recv_z.at[s, t]).wait()
+            here = rz.at[s, t, pl.ds(0, mj * L + JS)]
+            pltpu.make_async_copy(here, here, recv_z.at[s, t]).wait()
             sc[t, k] = whole(rz[s, t, mj * L:mj * L + JS, :]) * (1.0 / unit(limits[2])[1])
             for m in range(mj):
-                out[t * L:(t + 1) * L, m * 128:(m + 1) * 128] += (
+                out[starts[t]:starts[t] + L, m * 128:(m + 1) * 128] += (
                     whole(rz[s, t, m * L:(m + 1) * L, :]) * sc[t, k, pl.ds(z * mj + m, 1), :])
 
     grown = 0
-    for t in range(CHUNKS + 2):
-        if t < CHUNKS:
-            need = -(-((t + 1) * L + Q - 1) // Q)
+    for t in range(len(CHUNKS) + 2):
+        if t < len(CHUNKS):
+            need = -(-(starts[t] + CHUNKS[t] + Q - 1) // Q)
             build(grown, need)
             grown = need
             for q in (3, 1, 2, 0):
                 multiply(q, t)
-        if 0 <= t - 1 < CHUNKS:
+        if 0 <= t - 1 < len(CHUNKS):
             second(t - 1)
-        if 0 <= t - 2 < CHUNKS:
+        if 0 <= t - 2 < len(CHUNKS):
             third(t - 2)
-    for t in range(CHUNKS):
+    for t in range(len(CHUNKS)):
         fourth(t)
 
-    @pl.when(leads)
-    def _():
-        for k in range(2):
-            copy_h(k).wait_send()
-
     for k in range(2):
+        pl.when(jnp.logical_and(chip > 0, core == k))(copy_h(k).wait_send)
+
+    @pl.when(core == 0)
+    def _():
+        copy_v(0).wait_send()
+
+    for k in range(1, 3):
         copy_v(k).wait_send()
-    for t in range(CHUNKS):
+    for t in range(len(CHUNKS)):
         for k in range(6):
             copy_u(t, k).wait_send()
         for k in range(1, Z):
@@ -518,7 +551,8 @@
     mj = owned // width
     Z = n // 8
     R = rows // Q
-    L = LAGS // CHUNKS
+    T = len(CHUNKS)
+    L = max(CHUNKS)
     perm = np.zeros((width, width), np.float32)
     for core in range(2):
         for a in range(4):
@@ -529,31 +563,34 @@
     return pl.pallas_call(
         functools.partial(chip_kernel, n, mj),
         out_shape=jax.ShapeDtypeStruct((LAGS, owned), jnp.float32),
-        in_specs=[pl.BlockSpec(memory_space=pltpu.VMEM)] * 2,
+        in_specs=[pl.BlockSpec(memory_space=pltpu.HBM), pl.BlockSpec(memory_space=pltpu.VMEM)],
         out_specs=pl.BlockSpec(memory_space=pltpu.VMEM),
         scratch_shapes=[
+            pltpu.VMEM((rows, width), jnp.int32),
             pltpu.VMEM((2, Q // 2, R, 2 * width), jnp.bfloat16),
             pltpu.VMEM((2, 4, Q * JS, R), jnp.bfloat16),
             pltpu.VMEM((3, 4, Q * JS, R), jnp.bfloat16),
             pltpu.VMEM((4, 2, TAUS * JS, R), jnp.bfloat16),
             pltpu.VMEM((3, LAGS * JS, width), jnp.float32),
+            pltpu.VMEM((2, Q * (TAUS // Q - 1), width), jnp.bfloat16),
             pltpu.VMEM((Q * (TAUS // Q - 1), width), jnp.bfloat16),
-            pltpu.VMEM((Q * (TAUS // Q - 1), width), jnp.bfloat16),
-            pltpu.VMEM((CHUNKS, 6, tall, width), jnp.int16),
-            pltpu.VMEM((CHUNKS, 6, tall, width), jnp.int16),
-            pltpu.VMEM((Z, CHUNKS, mj * L + JS, width), jnp.int16),
-            pltpu.VMEM((Z, CHUNKS, mj * L + JS, width), jnp.int16),
-            pltpu.VMEM((CHUNKS, Z, JS, width), jnp.float32),
-            pltpu.SemaphoreType.DMA((2,)),
-            pltpu.SemaphoreType.DMA((2,)),
+            pltpu.VMEM((T, 6, tall, width), jnp.int16),
+            pltpu.VMEM((T, 6, tall, width), jnp.int16),
+            pltpu.VMEM((Z, T, mj * L + JS, width), jnp.int16),
+            pltpu.VMEM((Z, T, mj * L + JS, width), jnp.int16),
+            pltpu.VMEM((T, Z, JS, width), jnp.float32),
+            pltpu.SemaphoreType.DMA((1,)),
+            pltpu.SemaphoreType.REGULAR((max(2, Z - 2),)),
+            pltpu.SemaphoreType.DMA((3,)),
+            pltpu.SemaphoreType.DMA((3,)),
             pltpu.SemaphoreType.DMA((2,)),
             pltpu.SemaphoreType.DMA((1,)),
-            pltpu.SemaphoreType.DMA((CHUNKS, 6)),
-            pltpu.SemaphoreType.DMA((CHUNKS, 6)),
-            pltpu.SemaphoreType.DMA((Z, CHUNKS)),
-            pltpu.SemaphoreType.DMA((Z, CHUNKS)),
+            pltpu.SemaphoreType.DMA((T, 6)),
+            pltpu.SemaphoreType.DMA((T, 6)),
+            pltpu.SemaphoreType.DMA((Z, T)),
+            pltpu.SemaphoreType.DMA((Z, T)),
         ],
-        compiler_params=pltpu.CompilerParams(has_side_effects=True, collective_id=1, vmem_limit_bytes=56 * 1024 * 1024),
+        compiler_params=pltpu.CompilerParams(has_side_effects=True, collective_id=1, vmem_limit_bytes=24 * 1024 * 1024),
     )(samples, jnp.asarray(perm, jnp.bfloat16))
 
 

time: 49.3 us -> 43.5 us (0.88)
  Pallas kernels: 47 us -> 40.1 us
  local copies, waits for them, and re-layouts: 0.01 us -> 1.99 us
  matrix products: 2.11 us -> 1.16 us
    pallas_call x1, Pallas kernels: 47 us -> 40.1 us  [chip_lags(): pl.pallas_call(functools.partial(chip_kernel, n, mj), out_shape=jax.Shape...]
    unnamed x2 -> x6, local copies, waits for them, and re-layouts: 0.01 us -> 1.99 us
    dot_general x1, matrix products: 2.11 us -> 1.16 us  [on_device(): jnp.dot(jnp.asarray(table, jnp.float32), lagged, preferred_element_type=j...]
where the time goes in v2:
time: 43.5 us; the launch traced here: 43.3 us
  Pallas kernels  40.1 us (92%)
  local copies, waits for them, and re-layouts  1.99 us (5%)
  matrix products  1.16 us (3%)
    pallas_call x1, Pallas kernels, chip_lags(): pl.pallas_call(functools.partial(chip_kernel, n, mj), out_shape=jax.Shape...  40.1 us
    unnamed x6, local copies, waits for them, and re-layouts  1.99 us
    dot_general x1, matrix products, on_device(): jnp.dot(jnp.asarray(table, jnp.float32), lagged, preferred_element_type=j...  1.16 us

profile of v2, /device:TPU:0, one launch (start us, length us, event | category | flops | bytes accessed | tf_op | source)
XLA Modules:
  0.0 43.3 jit_solution(3859820793410780733)
XLA Ops:
  0.0 0.0 copy-start
  0.0 1.2 %copy-done = s32[2048,128]{1,0:T(8,128)S(1)} copy-done((s32[2048,128]{1,0:T(8,128)S(1)}, s32[2048,128]{1,0:T(8,128)}, u32[]{:S(2)}) %copy-start) | copy-done | bytes 1048600
  1.2 0.0 copy-start.1
  1.2 0.8 %copy-done.1 = bf16[128,128]{1,0:T(8,128)(2,1)S(1)} copy-done((bf16[128,128]{1,0:T(8,128)(2,1)S(1)}, bf16[128,128]{1,0:T(8,128)(2,1)}, u32[]{:S(2)}) %copy-start.1) | copy-done | bytes 32792
  2.0 0.0 copy-start.2
  2.0 40.1 %shard_map.37 = f32[128,512]{1,0:T(8,128)S(1)} custom-call(s32[2048,128]{1,0:T(8,128)S(1)} %copy-done, bf16[128,128]{1,0:T(8,128)(2,1)S(1)} %copy-done.1), custom_call_target="tpu_custom_call" | custom-call | tf_op jit(solution)/shard_map/pallas_call | solution.py:563
  42.1 0.0 copy-done.2
  42.1 1.2 %fusion = f32[256,512]{1,0:T(8,128)} fusion(f32[256,128]{1,0:T(8,128)S(1)} %copy-done.2, f32[128,512]{1,0:T(8,128)S(1)} %shard_map.37), kind=kOutput, calls=%fused_computation | convolution fusion | flops 100663296 | bytes 917504 | tf_op jit(solution)/shard_map/dot_general | solution.py:643
Async XLA Ops:
  0.0 1.2 %copy-start = (s32[2048,128]{1,0:T(8,128)S(1)}, s32[2048,128]{1,0:T(8,128)}, u32[]{:S(2)}) copy-start(s32[2048,128]{1,0:T(8,128)} %samples.1) | copy-start | bytes 3145732
  1.2 0.8 %copy-start.1 = (bf16[128,128]{1,0:T(8,128)(2,1)S(1)}, bf16[128,128]{1,0:T(8,128)(2,1)}, u32[]{:S(2)}) copy-start(bf16[128,128]{1,0:T(8,128)(2,1)} %constant.4.clone.perm) | copy-start | bytes 98308
  2.0 40.1 %copy-start.2 = (f32[256,128]{1,0:T(8,128)S(1)}, f32[256,128]{1,0:T(8,128)}, u32[]{:S(2)}) copy-start(f32[256,128]{1,0:T(8,128)} %constant.5.clone) | copy-start | bytes 393220

commit v3 on v2

--- a/solution.py
+++ b/solution.py
@@ -14,7 +14,7 @@
 TAUS = LAGS + Q
 OUT_ROWS = (LAGS + 1) * JS
 TILE = OUT_ROWS // 3
-CHUNKS = (32, 32, 32, 16, 16)
+CHUNKS = (32, 32, 32, 32)
 MESH = pl.DeviceIdType.MESH
 
 
@@ -398,35 +398,35 @@
     for k in range(2):
         pl.when(jnp.logical_and(chip > 0, core == k))(copy_h(k).start)
 
-    @pl.when(chip == chips - 1)
-    def _():
-        hr[...] = jnp.zeros(hr.shape, hr.dtype)
-
-    @pl.when(chip < chips - 1)
-    def _():
-        pltpu.make_async_copy(hr, hr, recv_h.at[0]).wait()
-
-    edge = lax.dot_general(
-        perm[pl.ds(pl.multiple_of(core * 4 * JS, 4 * JS), 4 * JS), :], hr[...],
-        (((1,), (1,)), ((), ())), preferred_element_type=jnp.float32)
-    for q in range(Q):
-        moved = edge if q == 0 else pltpu.roll(edge, 128 - q * (reach - 1), 1)
-        for a in range(4):
-            tb[2, a, q * JS:(q + 1) * JS, :] = moved[a * JS:(a + 1) * JS, :].astype(jnp.bfloat16)
-
     for k in range(2):
         there = (vbuf, tb)[k].at[1 - core]
         pltpu.make_async_copy(there, there, recv_v.at[k + 1]).wait()
 
-    def build(first, last):
-        def one(a, carry):
-            for d in range(2):
-                pair = jnp.concatenate([tb[d, a], tb[d + 1, a]], axis=1)
-                for s in range(first, last):
-                    ut[a, d, s * Q * JS:(s + 1) * Q * JS, :] = pair[:, s:s + R]
-            return carry
-
-        lax.fori_loop(0, 4, one, 0)
+    places = [(x, 1 - x)[q % 2] + 2 * (y, 1 - y)[q // 2] for q in range(4)]
+
+    def build(q, d, s):
+        if s == 0:
+            ut[q, d, 0:Q * JS, :] = tb[d, places[q]]
+        else:
+            pair = jnp.concatenate([tb[d, places[q]], tb[d + 1, places[q]]], axis=1)
+            ut[q, d, s * Q * JS:(s + 1) * Q * JS, :] = pair[:, s:s + R]
+
+    def head():
+        @pl.when(chip == chips - 1)
+        def _():
+            hr[...] = jnp.zeros(hr.shape, hr.dtype)
+
+        @pl.when(chip < chips - 1)
+        def _():
+            pltpu.make_async_copy(hr, hr, recv_h.at[0]).wait()
+
+        edge = lax.dot_general(
+            perm[pl.ds(pl.multiple_of(core * 4 * JS, 4 * JS), 4 * JS), :], hr[...],
+            (((1,), (1,)), ((), ())), preferred_element_type=jnp.float32)
+        for q in range(Q):
+            moved = edge if q == 0 else pltpu.roll(edge, 128 - q * (reach - 1), 1)
+            for a in range(4):
+                tb[2, a, q * JS:(q + 1) * JS, :] = moved[a * JS:(a + 1) * JS, :].astype(jnp.bfloat16)
 
     def copy_u(t, k):
         rows_u = pl.ds(0, (CHUNKS[t] // 2 + 1) * JS)
@@ -455,26 +455,21 @@
         half = CHUNKS[t] * JS // 2
         return starts[t] * JS + h * half, half
 
-    def multiply(q, t):
-        a = (x, 1 - x)[q % 2] + 2 * (y, 1 - y)[q // 2]
+    def products(q, t, blocks):
         full = []
         for h in range(2):
             r0, half = rows_of(t, h)
             left = jnp.concatenate(
-                [ut[a, d, r0 + 2 * JS * e:r0 + 2 * JS * e + half + JS, :] for d in range(2) for e in range(Q // 2)], axis=1)
-            part = jnp.dot(left, vbuf[...].reshape(Q * R, 256), preferred_element_type=jnp.float32)
+                [ut[q, d, r0 + 2 * JS * e:r0 + 2 * JS * e + half + JS, :] for d in blocks for e in range(Q // 2)], axis=1)
+            right = vbuf[blocks[0]:blocks[-1] + 1].reshape(len(blocks) * Q // 2 * R, 256)
+            part = jnp.dot(left, right, preferred_element_type=jnp.float32)
             full.append(part[0:half, 0:128] + part[JS:half + JS, 128:256])
+        return full
+
+    def keep(k, t, full):
         for h in range(2):
             r0, half = rows_of(t, h)
-            if q == 3 or q == h + 1:
-                send(t, 2 * h + (0 if q == 3 else 1), full[h], limits[0])
-            else:
-                acc[q, r0:r0 + half, :] = full[h]
-
-    def second(t):
-        for h in range(2):
-            r0, half = rows_of(t, h)
-            send(t, 4 + h, acc[2 - h, r0:r0 + half, :] + received(t, 2 * h, limits[0]), limits[1])
+            acc[k, r0:r0 + half, :] = full[h]
 
     def copy_z(t, k):
         d = (z + k) % Z
@@ -514,19 +509,58 @@
                 out[starts[t]:starts[t] + L, m * 128:(m + 1) * 128] += (
                     whole(rz[s, t, m * L:(m + 1) * L, :]) * sc[t, k, pl.ds(z * mj + m, 1), :])
 
-    grown = 0
-    for t in range(len(CHUNKS) + 2):
-        if t < len(CHUNKS):
-            need = -(-(starts[t] + CHUNKS[t] + Q - 1) // Q)
-            build(grown, need)
-            grown = need
-            for q in (3, 1, 2, 0):
-                multiply(q, t)
-        if 0 <= t - 1 < len(CHUNKS):
+    T = len(CHUNKS)
+
+    def some(pieces, t):
+        for piece in pieces[t * len(pieces) // T:(t + 1) * len(pieces) // T]:
+            build(*piece)
+
+    shifts = range(reach)
+    for s in shifts:
+        build(3, 0, s)
+    for t in range(T):
+        some([(q, 0, s) for q in (1, 2, 0) for s in shifts], t)
+        keep(1, t, products(3, t, (0,)))
+    head()
+    for s in shifts:
+        build(3, 1, s)
+    needed = [0] + [-(-(starts[t] + CHUNKS[t] + Q - 1) // Q) for t in range(T)]
+
+    def outer(t):
+        for q in (1, 2, 0):
+            for s in range(needed[t], needed[t + 1]):
+                build(q, 1, s)
+        full = products(3, t, (1,))
+        for h in range(2):
+            r0, half = rows_of(t, h)
+            send(t, 2 * h, acc[1, r0:r0 + half, :] + full[h], limits[0])
+
+    def beside(t):
+        one = products(1, t, (0, 1))
+        two = products(2, t, (0, 1))
+        send(t, 1, one[0], limits[0])
+        send(t, 3, two[1], limits[0])
+        for h in range(2):
+            r0, half = rows_of(t, h)
+            acc[2, r0:r0 + half, :] = (two[0], one[1])[h]
+
+    def second(t):
+        for h in range(2):
+            r0, half = rows_of(t, h)
+            send(t, 4 + h, acc[2, r0:r0 + half, :] + received(t, 2 * h, limits[0]), limits[1])
+
+    for t in range(T + 1):
+        if t < T:
+            outer(t)
+        if t > 0:
+            keep(0, t - 1, products(0, t - 1, (0, 1)))
             second(t - 1)
-        if 0 <= t - 2 < len(CHUNKS):
+        if t < T:
+            beside(t)
+        if t > 1:
             third(t - 2)
-    for t in range(len(CHUNKS)):
+    third(T - 1)
+    for t in range(T):
         fourth(t)
 
     for k in range(2):
@@ -590,7 +624,7 @@
             pltpu.SemaphoreType.DMA((Z, T)),
             pltpu.SemaphoreType.DMA((Z, T)),
         ],
-        compiler_params=pltpu.CompilerParams(has_side_effects=True, collective_id=1, vmem_limit_bytes=24 * 1024 * 1024),
+        compiler_params=pltpu.CompilerParams(has_side_effects=True, collective_id=1, vmem_limit_bytes=54016 * 1024),
     )(samples, jnp.asarray(perm, jnp.bfloat16))
 
 

time: 43.5 us -> 39.3 us (0.903)
  Pallas kernels: 40.1 us -> 37.2 us
  local copies, waits for them, and re-layouts: 1.99 us -> 0.76 us
    pallas_call x1, Pallas kernels: 40.1 us -> 37.2 us  [chip_lags(): pl.pallas_call(functools.partial(chip_kernel, n, mj), out_shape=jax.Shape...]
    unnamed x6 -> x4, local copies, waits for them, and re-layouts: 1.99 us -> 0.76 us
where the time goes in v3:
time: 39.3 us; the launch traced here: 39.1 us
  Pallas kernels  37.2 us (95%)
  matrix products  1.16 us (3%)
  local copies, waits for them, and re-layouts  0.76 us (2%)
    pallas_call x1, Pallas kernels, chip_lags(): pl.pallas_call(functools.partial(chip_kernel, n, mj), out_shape=jax.Shape...  37.2 us
    dot_general x1, matrix products, on_device(): jnp.dot(jnp.asarray(table, jnp.float32), lagged, preferred_element_type=j...  1.16 us

profile of v3, /device:TPU:0, one launch (start us, length us, event | category | flops | bytes accessed | tf_op | source)
XLA Modules:
  0.0 39.1 jit_solution(10760098262141012853)
XLA Ops:
  0.0 0.0 copy-start
  0.0 0.8 %copy-done = bf16[128,128]{1,0:T(8,128)(2,1)S(1)} copy-done((bf16[128,128]{1,0:T(8,128)(2,1)S(1)}, bf16[128,128]{1,0:T(8,128)(2,1)}, u32[]{:S(2)}) %copy-start) | copy-done | bytes 32792
  0.8 0.0 copy-start.1
  0.8 37.2 %shard_map.37 = f32[128,512]{1,0:T(8,128)S(1)} custom-call(s32[2048,128]{1,0:T(8,128)} %samples.1, bf16[128,128]{1,0:T(8,128)(2,1)S(1)} %copy-done), custom_call_target="tpu_custom_call" | custom-call | tf_op jit(solution)/shard_map/pallas_call | solution.py:597
  37.9 0.0 copy-done.1
  37.9 1.2 %fusion = f32[256,512]{1,0:T(8,128)} fusion(f32[256,128]{1,0:T(8,128)S(1)} %copy-done.1, f32[128,512]{1,0:T(8,128)S(1)} %shard_map.37), kind=kOutput, calls=%fused_computation | convolution fusion | flops 100663296 | bytes 917504 | tf_op jit(solution)/shard_map/dot_general | solution.py:677
Async XLA Ops:
  0.0 0.8 %copy-start = (bf16[128,128]{1,0:T(8,128)(2,1)S(1)}, bf16[128,128]{1,0:T(8,128)(2,1)}, u32[]{:S(2)}) copy-start(bf16[128,128]{1,0:T(8,128)(2,1)} %constant.4.clone.perm) | copy-start | bytes 98308
  0.8 37.2 %copy-start.1 = (f32[256,128]{1,0:T(8,128)S(1)}, f32[256,128]{1,0:T(8,128)}, u32[]{:S(2)}) copy-start(f32[256,128]{1,0:T(8,128)} %constant.5.clone) | copy-start | bytes 393220

commit v4 on v3

--- a/solution.py
+++ b/solution.py
@@ -390,13 +390,16 @@
             src_ref=hs.at[k], dst_ref=hr, send_sem=send_h.at[k], recv_sem=recv_h.at[0],
             device_id=(me - 2,), device_id_type=MESH)
 
+    for k in range(2):
+        pl.when(jnp.logical_and(x == 1, core == k))(copy_h(k).start)
+
     for stage in range(rounds):
         pl.semaphore_wait(heard.at[stage], around)
         if stage < rounds - 1:
             tell(stage + 1)
 
     for k in range(2):
-        pl.when(jnp.logical_and(chip > 0, core == k))(copy_h(k).start)
+        pl.when(jnp.logical_and(jnp.logical_and(chip > 0, x == 0), core == k))(copy_h(k).start)
 
     for k in range(2):
         there = (vbuf, tb)[k].at[1 - core]
@@ -522,12 +525,10 @@
         some([(q, 0, s) for q in (1, 2, 0) for s in shifts], t)
         keep(1, t, products(3, t, (0,)))
     head()
-    for s in shifts:
-        build(3, 1, s)
     needed = [0] + [-(-(starts[t] + CHUNKS[t] + Q - 1) // Q) for t in range(T)]
 
     def outer(t):
-        for q in (1, 2, 0):
+        for q in (3, 1, 2, 0):
             for s in range(needed[t], needed[t + 1]):
                 build(q, 1, s)
         full = products(3, t, (1,))

time: 39.3 us -> 39.2 us (level)
  no operation moved by 1% of the time
where the time goes in v4:
time: 39.2 us; the launch traced here: 39 us
  Pallas kernels  37 us (94%)
  matrix products  1.16 us (3%)
  local copies, waits for them, and re-layouts  0.76 us (2%)
    pallas_call x1, Pallas kernels, chip_lags(): pl.pallas_call(functools.partial(chip_kernel, n, mj), out_shape=jax.Shape...  37 us
    dot_general x1, matrix products, on_device(): jnp.dot(jnp.asarray(table, jnp.float32), lagged, preferred_element_type=j...  1.16 us

profile of v4, /device:TPU:0, one launch (start us, length us, event | category | flops | bytes accessed | tf_op | source)
XLA Modules:
  0.0 39.0 jit_solution(14409704317675682532)
XLA Ops:
  0.0 0.0 copy-start
  0.0 0.8 %copy-done = bf16[128,128]{1,0:T(8,128)(2,1)S(1)} copy-done((bf16[128,128]{1,0:T(8,128)(2,1)S(1)}, bf16[128,128]{1,0:T(8,128)(2,1)}, u32[]{:S(2)}) %copy-start) | copy-done | bytes 32792
  0.8 0.0 copy-start.1
  0.8 37.0 %shard_map.37 = f32[128,512]{1,0:T(8,128)S(1)} custom-call(s32[2048,128]{1,0:T(8,128)} %samples.1, bf16[128,128]{1,0:T(8,128)(2,1)S(1)} %copy-done), custom_call_target="tpu_custom_call" | custom-call | tf_op jit(solution)/shard_map/pallas_call | solution.py:598
  37.8 0.0 copy-done.1
  37.8 1.2 %fusion = f32[256,512]{1,0:T(8,128)} fusion(f32[256,128]{1,0:T(8,128)S(1)} %copy-done.1, f32[128,512]{1,0:T(8,128)S(1)} %shard_map.37), kind=kOutput, calls=%fused_computation | convolution fusion | flops 100663296 | bytes 917504 | tf_op jit(solution)/shard_map/dot_general | solution.py:678
Async XLA Ops:
  0.0 0.8 %copy-start = (bf16[128,128]{1,0:T(8,128)(2,1)S(1)}, bf16[128,128]{1,0:T(8,128)(2,1)}, u32[]{:S(2)}) copy-start(bf16[128,128]{1,0:T(8,128)(2,1)} %constant.4.clone.perm) | copy-start | bytes 98308
  0.8 37.0 %copy-start.1 = (f32[256,128]{1,0:T(8,128)S(1)}, f32[256,128]{1,0:T(8,128)}, u32[]{:S(2)}) copy-start(f32[256,128]{1,0:T(8,128)} %constant.5.clone) | copy-start | bytes 393220
